TPU v7x, 128 devices: a whole 4x4x4 slice. The times are simulated.
128 devices in a mesh: row: 8 (over z, core), col: 16 (over y, x).
Axes of the slice: x: 4, y: 4, z: 4, core: 2. Of those that a mesh axis runs over, the one named last changes fastest.
Arguments:
- real_feats: bfloat16 [16384, 2048], P(('row', 'col')), may hold values from 0 to 8, as said below
- fake_feats: bfloat16 [16384, 2048], P(('row', 'col')), may hold values from 0 to 8, as said below
Outputs:
- proof_real: float32 [16384], P(('row', 'col'))
- proof_fake: float32 [16384], P(('row', 'col'))
- kid: float32 [], replicated
Inputs may be any that keep to these rules, and one draw needn't show every extreme that they name: `real_feats`: nonnegative features. `fake_feats`: nonnegative features.
All inputs are finite; a program needn't handle non-finite values.
Results may differ from a plain program's by a relative error of at most 0.0003.
Values may be sent and summed in bfloat16 or wider, within the bound.
No kernel may reach another device: no remote copies, remote signals or barrier semaphores. Data moves between devices by JAX's collectives and lax.ppermute only.
A program may use at most 128 MiB of HBM per device.

v0:
```python
import jax
import jax.numpy as jnp
from jax import lax
from jax.sharding import Mesh
from jax.sharding import PartitionSpec as P

ROW = ("row_0", "row_1")
COL = ("col_0", "col_1")
ROW_COL = ("row_0", "row_1", "col_0", "col_1")


def in_one_piece(arrays, axis, dim, along):
    both = jnp.concatenate(arrays, axis=along)
    out, at, finished = (lax.all_gather(both, axis, axis=dim, tiled=True), 0, [])
    for a in arrays:
        finished.append(lax.slice_in_dim(out, at, at + a.shape[along], axis=along))
        at += a.shape[along]
    return tuple(finished)


def split_up(value, dim, length):
    before, after = (value.shape[:dim], value.shape[dim + 1 :])
    return jnp.moveaxis(value.reshape(*before, length, -1, *after), dim, 0)


def sum_at_owner(value, axis, dim):
    length = lax.axis_size(axis)
    blocks = lax.all_to_all(split_up(value, dim, length), axis, 0, 0, tiled=True)
    return jnp.sum(blocks, axis=0)


def over_axes(value, axes):
    for axis in axes:
        value = lax.psum(value, axis)
    return value


def kernel_block(left, right, width):
    inner = lax.dot_general(
        left, right, (((1,), (1,)), ((), ())), preferred_element_type=jnp.float32
    )
    shifted = inner / width + 1.0
    return shifted * shifted * shifted


def shards(real_feats, fake_feats):
    rows_dev = real_feats.shape[0]
    width = real_feats.shape[1]
    n_row = lax.axis_size(ROW)
    n_col = lax.axis_size(COL)
    total = float(rows_dev * n_row * n_col)
    row_count = rows_dev * n_col
    col_count = rows_dev * n_row
    col_real, col_fake = (
        lax.all_gather(real_feats, ROW, axis=0, tiled=True),
        lax.all_gather(fake_feats, ROW, axis=0, tiled=True),
    )
    places = jnp.arange(col_count, dtype=jnp.int32)
    col_ids = places // rows_dev * row_count + lax.axis_index(COL) * rows_dev + places % rows_dev
    row_base = lax.axis_index(ROW) * row_count
    rows_real, rows_fake = in_one_piece((real_feats, fake_feats), COL, 0, 1)
    count = rows_real.shape[0]
    row_ids = row_base + jnp.arange(count, dtype=jnp.int32)
    off_diag = row_ids[:, None] != col_ids[None, :]
    same_real = jnp.where(off_diag, kernel_block(rows_real, col_real, width), 0.0)
    same_fake = jnp.where(off_diag, kernel_block(rows_fake, col_fake, width), 0.0)
    cross = kernel_block(rows_real, col_fake, width)
    first = jnp.sum(same_real, axis=1) / (total - 1.0) - jnp.sum(cross, axis=1) / total
    second = jnp.sum(same_fake, axis=1) / (total - 1.0)
    column = jnp.sum(cross, axis=0) / total
    first, second, column = (first, second, column)
    owned_first, owned_second = (sum_at_owner(first, COL, 0), sum_at_owner(second, COL, 0))
    owned_column = sum_at_owner(column, ROW, 0)
    proof_fake = owned_second - owned_column
    kid = over_axes(jnp.sum(owned_first) + jnp.sum(proof_fake), ROW_COL) / total
    return (owned_first, proof_fake, kid)


def solution(mesh):
    split = Mesh(mesh.devices.reshape(4, 2, 4, 4), ("row_0", "row_1", "col_0", "col_1"))
    placed = (P(ROW_COL, None), P(ROW_COL, None))
    return jax.shard_map(
        shards,
        mesh=split,
        in_specs=placed,
        out_specs=(P(ROW_COL), P(ROW_COL), P()),
        check_vma=False,
    )
```

profile of v0, /device:TPU:0, one launch (start us, length us, event | category | flops | bytes accessed | tf_op | source)
XLA Modules:
  0.0 272.9 jit_solution(2580525084667997164)
XLA Ops:
  7.2 0.0 all-gather.8.cloned.1.call-start
  7.2 0.7 all-gather.8.cloned.1.call-update
  7.9 0.0 all-gather.4.cloned.1.call-start
  7.9 2.4 pad_maximum_fusion
  10.3 0.0 all-gather.4.cloned.1.call-update
  10.3 0.0 all-gather.6.cloned.1.call-start
  10.4 0.7 all-gather.6.cloned.1.call-update
  11.1 33.4 %all-gather.8.cloned.1.call-done = bf16[1024,2048]{1,0:T(8,128)(2,1)} async-done(((bf16[128,2048]{1,0:T(8,128)(2,1)}), bf16[1024,2048]{1,0:T(8,128)(2,1)}) %all-gather.8.cloned.1.call-update) | async-done | bytes 4194320 | tf_op jit(solution)/shard_map/all_gather | solution.py:56
  44.5 113.0 %all-gather.4.cloned.1.call-done = bf16[2048,4096]{1,0:T(8,128)(2,1)} async-done(((bf16[128,4096]{1,0:T(8,128)(2,1)}), bf16[2048,4096]{1,0:T(8,128)(2,1)}) %all-gather.4.cloned.1.call-update) | async-done | bytes 16777232 | tf_op jit(solution)/shard_map/all_gather | solution.py:14
  157.5 13.0 %fusion.8 = (f32[1024]{0:T(1024)S(1)}, f32[2048]{0:T(1024)S(1)}) fusion(bf16[1024,2048]{1,0:T(8,128)(2,1)} %all-gather.8.cloned.1.call-done, bf16[2048,4096]{1,0:T(8,128)(2,1)} %all-gather.4.cloned.1.call-done), kind=kOutput, calls=%fused_computation.13 | convolution fusion | flops 8602514432 | bytes 12595200 | tf_op jit(solution)/shard_map/dot_general | solution.py:39
  170.5 0.6 broadcast_multiply_fusion.1
  171.1 4.4 %all-to-all-start.2 = ((f32[8,1,128]{2,1,0:T(1,128)}), f32[8,1,128]{2,1,0:T(1,128)S(1)}, u32[]{:S(2)}, u32[]{:S(2)}) async-start(f32[8,1,128]{2,1,0:T(1,128)} %bitcast.4), calls=%async_computation.2 | async-start | bytes 8192 | tf_op jit(solution)/shard_map/all_to_all | solution.py:28
  175.5 13.4 %fusion.1 = f32[2048]{0:T(1024)S(1)} fusion(bf16[1024,2048]{1,0:T(8,128)(2,1)} %all-gather.8.cloned.1.call-done, bf16[2048,4096]{1,0:T(8,128)(2,1)} %all-gather.4.cloned.1.call-done, s32[2048]{0:T(1024)S(1)} %iota_add_fusion, s32[1024]{0:T(1024)S(1)} %fusion.22), kind=kOutput, calls=%fused_computation.6 | convolution fusion | flops 8604612608 | bytes 12603392 | tf_op jit(solution)/shard_map/dot_general | solution.py:39
  189.0 2.3 all-gather.6.cloned.1.call-done
  191.3 13.3 %fusion = f32[2048]{0:T(1024)S(1)} fusion(bf16[1024,2048]{1,0:T(8,128)(2,1)} %all-gather.6.cloned.1.call-done, bf16[2048,4096]{1,0:T(8,128)(2,1)} %all-gather.4.cloned.1.call-done, s32[2048]{0:T(1024)S(1)} %iota_add_fusion, s32[1024]{0:T(1024)S(1)} %fusion.22), kind=kOutput, calls=%fused_computation.5 | convolution fusion | flops 8604612608 | bytes 12603392 | tf_op jit(solution)/shard_map/dot_general | solution.py:39
  204.6 0.6 broadcast_multiply_fusion
  205.2 0.0 all-to-all-done.2
  205.2 6.8 %all-to-all-start.1 = ((f32[16,1,128]{2,1,0:T(1,128)}), f32[16,1,128]{2,1,0:T(1,128)S(1)}, u32[]{:S(2)}, u32[]{:S(2)}) async-start(f32[16,1,128]{2,1,0:T(1,128)} %bitcast.2), calls=%async_computation.1 | async-start | bytes 16384 | tf_op jit(solution)/shard_map/all_to_all | solution.py:28
  212.0 0.6 multiply_subtract_fusion
  212.6 6.8 %all-to-all-done.1 = f32[16,1,128]{2,1,0:T(1,128)S(1)} async-done(((f32[16,1,128]{2,1,0:T(1,128)}), f32[16,1,128]{2,1,0:T(1,128)S(1)}, u32[]{:S(2)}, u32[]{:S(2)}) %all-to-all-start.1) | async-done | bytes 8224 | tf_op jit(solution)/shard_map/all_to_all | solution.py:28
  219.4 3.4 %all-to-all-start = ((f32[16,1,128]{2,1,0:T(1,128)}), f32[16,1,128]{2,1,0:T(1,128)S(1)}, u32[]{:S(2)}, u32[]{:S(2)}) async-start(f32[16,1,128]{2,1,0:T(1,128)} %bitcast), calls=%async_computation | async-start | bytes 16384 | tf_op jit(solution)/shard_map/all_to_all | solution.py:28
  222.9 7.5 %all-to-all-done = f32[16,1,128]{2,1,0:T(1,128)S(1)} async-done(((f32[16,1,128]{2,1,0:T(1,128)}), f32[16,1,128]{2,1,0:T(1,128)S(1)}, u32[]{:S(2)}, u32[]{:S(2)}) %all-to-all-start) | async-done | bytes 8224 | tf_op jit(solution)/shard_map/all_to_all | solution.py:28
  230.4 0.6 fusion.24
  231.0 1.2 fusion.25
  233.5 9.0 %psum.28 = f32[]{:T(128)} all-reduce(f32[]{:T(128)S(6)} %add.79), channel_id=1, replica_groups=mesh['row_0'=4,'row_1'=2,'col_0'=4,'col_1'=4] {'row_0'}, use_global_device_ids=true, to_apply=%region_9.10 | all-reduce | flops 1 | bytes 8 | tf_op jit(solution)/shard_map/psum | solution.py:34
  242.5 3.1 %psum.29 = f32[]{:T(128)} all-reduce(f32[]{:T(128)} %psum.28), channel_id=1, replica_groups=mesh['row_0'=4,'row_1'=2,'col_0'=4,'col_1'=4] {'row_1'}, use_global_device_ids=true, to_apply=%region_10.11 | all-reduce | flops 1 | bytes 8 | tf_op jit(solution)/shard_map/psum | solution.py:34
  245.6 9.5 %psum.30 = f32[]{:T(128)} all-reduce(f32[]{:T(128)} %psum.29), channel_id=1, replica_groups=mesh['row_0'=4,'row_1'=2,'col_0'=4,'col_1'=4] {'col_0'}, use_global_device_ids=true, to_apply=%region_11.12 | all-reduce | flops 1 | bytes 8 | tf_op jit(solution)/shard_map/psum | solution.py:34
  255.1 9.5 %psum.31 = f32[]{:T(128)} all-reduce(f32[]{:T(128)} %psum.30), channel_id=1, replica_groups=mesh['row_0'=4,'row_1'=2,'col_0'=4,'col_1'=4] {'col_1'}, use_global_device_ids=true, to_apply=%region_12.13 | all-reduce | flops 1 | bytes 8 | tf_op jit(solution)/shard_map/psum | solution.py:34
  (4 shorter events, 0.1 us)
Async XLA Ops:
  7.2 37.3 %all-gather.8.cloned.1.call-start = ((), (), s32[]{:S(2)}) async-start(), calls=%async_computation.5 | async-start | bytes 4718592 | tf_op jit(solution)/shard_map/all_gather | solution.py:56
  7.9 149.6 %all-gather.4.cloned.1.call-start = ((), (), s32[]{:S(2)}) async-start(), calls=%async_computation.3 | async-start | bytes 17825792 | tf_op jit(solution)/shard_map/all_gather | solution.py:14
  10.3 181.0 %all-gather.6.cloned.1.call-start = ((), (), s32[]{:S(2)}) async-start(), calls=%async_computation.4 | async-start | bytes 4718592 | tf_op jit(solution)/shard_map/all_gather | solution.py:55
  171.1 34.1 %all-to-all-start.2 = ((f32[8,1,128]{2,1,0:T(1,128)}), f32[8,1,128]{2,1,0:T(1,128)S(1)}, u32[]{:S(2)}, u32[]{:S(2)}) async-start(f32[8,1,128]{2,1,0:T(1,128)} %bitcast.4), calls=%async_computation.2 | async-start | bytes 8192 | tf_op jit(solution)/shard_map/all_to_all | solution.py:28
  205.2 14.2 %all-to-all-start.1 = ((f32[16,1,128]{2,1,0:T(1,128)}), f32[16,1,128]{2,1,0:T(1,128)S(1)}, u32[]{:S(2)}, u32[]{:S(2)}) async-start(f32[16,1,128]{2,1,0:T(1,128)} %bitcast.2), calls=%async_computation.1 | async-start | bytes 16384 | tf_op jit(solution)/shard_map/all_to_all | solution.py:28
  219.4 10.9 %all-to-all-start = ((f32[16,1,128]{2,1,0:T(1,128)}), f32[16,1,128]{2,1,0:T(1,128)S(1)}, u32[]{:S(2)}, u32[]{:S(2)}) async-start(f32[16,1,128]{2,1,0:T(1,128)} %bitcast), calls=%async_computation | async-start | bytes 16384 | tf_op jit(solution)/shard_map/all_to_all | solution.py:28
Sparse Core Ops, SparseCore 0:
  9.7 34.7 all-gather.7
  46.6 110.8 all-gather.3
  159.2 32.0 all-gather.5
where the time goes:
time: 273 us
  waiting for transfers between devices  164 us (60%)
  matrix products  39.7 us (15%)
  blocking collectives  31.1 us (11%)
  between operations  16.9 us (6%)
  starting transfers between devices  14.7 us (5%)
  other arithmetic  5.99 us (2%)
    all_gather x1, waiting for transfers between devices, in_one_piece(): lax.all_gather(both, axis, axis=dim, tiled=True)  113 us
    dot_general x3, matrix products, kernel_block(): lax.dot_general(left, right, (((1,), (1,)), ((), ())), preferred_element_...  39.7 us
    all_gather x1, waiting for transfers between devices, shards(): lax.all_gather(fake_feats, ROW, axis=0, tiled=True)  33.4 us
    psum x4, blocking collectives, over_axes(): value = lax.psum(value, axis)  31.1 us
    all_to_all x3, starting transfers between devices, sum_at_owner(): lax.all_to_all(split_up(value, dim, length), axis, 0, 0, tiled=True)  14.6 us
    all_to_all x3, waiting for transfers between devices, sum_at_owner(): lax.all_to_all(split_up(value, dim, length), axis, 0, 0, tiled=True)  14.3 us
  transfers between devices with their start and end apart: 6, of which 5 were waited for; matrix products, arithmetic and copies ran while one was open for 16% of the time, Pallas kernels for 0%

commit v1 on v0

--- a/solution.py
+++ b/solution.py
@@ -51,9 +51,16 @@
     total = float(rows_dev * n_row * n_col)
     row_count = rows_dev * n_col
     col_count = rows_dev * n_row
+
+    def get_the_numbers(buf):
+        return jnp.concatenate(
+            lax.all_to_all(jnp.stack([buf for _ in range(lax.axis_size(ROW))], axis=0), ROW, 0, 0),
+            axis=0,
+        )
+
     col_real, col_fake = (
         lax.all_gather(real_feats, ROW, axis=0, tiled=True),
-        lax.all_gather(fake_feats, ROW, axis=0, tiled=True),
+        get_the_numbers(fake_feats),
     )
     places = jnp.arange(col_count, dtype=jnp.int32)
     col_ids = places // rows_dev * row_count + lax.axis_index(COL) * rows_dev + places % rows_dev

time: 273 us -> 240 us (0.88)
  waiting for transfers between devices: 164 us -> 122 us
  starting transfers between devices: 14.7 us -> 20.1 us
  local copies, waits for them, and re-layouts: 0 us -> 3.55 us
    all_gather x1, waiting for transfers between devices: 113 us -> 55.4 us  [in_one_piece(): lax.all_gather(both, axis, axis=dim, tiled=True)]
    all_to_all x0 -> x1, waiting for transfers between devices: none -> 49 us  [get_the_numbers(): lax.all_to_all(jnp.stack([buf for _ in range(lax.axis_size(ROW))], axis=0...]
    all_gather x1 -> x0, waiting for transfers between devices: 33.4 us -> none  [shards(): lax.all_gather(fake_feats, ROW, axis=0, tiled=True)]
    all_to_all x0 -> x1, starting transfers between devices: none -> 5.43 us  [get_the_numbers(): lax.all_to_all(jnp.stack([buf for _ in range(lax.axis_size(ROW))], axis=0...]
    another operation x0 -> x1, local copies, waits for them, and re-layouts: none -> 3.55 us  [get_the_numbers(): jnp.stack([buf for _ in range(lax.axis_size(ROW))], axis=0)]
  transfers between devices with their start and end apart: 6 -> 6, of which waited for: 5 -> 5; matrix products, arithmetic and copies ran while one was open for 16% -> 19% of each run, Pallas kernels for 0% -> 0%
where the time goes in v1:
time: 240 us; the launch traced here: 239 us
  waiting for transfers between devices  122 us (51%)
  matrix products  39.7 us (17%)
  blocking collectives  31.1 us (13%)
  starting transfers between devices  20.1 us (8%)
  between operations  17.2 us (7%)
  other arithmetic  5.97 us (2%)
  local copies, waits for them, and re-layouts  3.55 us (1%)
    all_gather x1, waiting for transfers between devices, in_one_piece(): lax.all_gather(both, axis, axis=dim, tiled=True)  55.4 us
    all_to_all x1, waiting for transfers between devices, get_the_numbers(): lax.all_to_all(jnp.stack([buf for _ in range(lax.axis_size(ROW))], axis=0...  49 us
    dot_general x3, matrix products, kernel_block(): lax.dot_general(left, right, (((1,), (1,)), ((), ())), preferred_element_...  39.7 us
    psum x4, blocking collectives, over_axes(): value = lax.psum(value, axis)  31.1 us
    all_to_all x3, starting transfers between devices, sum_at_owner(): lax.all_to_all(split_up(value, dim, length), axis, 0, 0, tiled=True)  14.6 us
    all_to_all x3, waiting for transfers between devices, sum_at_owner(): lax.all_to_all(split_up(value, dim, length), axis, 0, 0, tiled=True)  14.3 us
    all_to_all x1, starting transfers between devices, get_the_numbers(): lax.all_to_all(jnp.stack([buf for _ in range(lax.axis_size(ROW))], axis=0...  5.43 us
  transfers between devices with their start and end apart: 6, of which 5 were waited for; matrix products, arithmetic and copies ran while one was open for 19% of the time, Pallas kernels for 0%

profile of v1, /device:TPU:0, one launch (start us, length us, event | category | flops | bytes accessed | tf_op | source)
XLA Modules:
  0.0 239.4 jit_solution(3388679062071986)
XLA Ops:
  7.2 0.0 all-gather.3.cloned.1.call-start
  7.2 2.3 pad_maximum_fusion
  9.5 0.0 all-gather.3.cloned.1.call-update
  9.6 3.5 %stack.2 = bf16[8,128,2048]{2,1,0:T(8,128)(2,1)} broadcast(bf16[128,2048]{1,0:T(8,128)(2,1)} %param.3), dimensions={1,2} | broadcast | bytes 4718592 | tf_op jit(solution)/shard_map/stack | solution.py:57
  13.1 5.4 %all-to-all-start = ((bf16[8,128,2048]{2,1,0:T(8,128)(2,1)}), bf16[8,128,2048]{2,1,0:T(8,128)(2,1)}, u32[]{:S(2)}, u32[]{:S(2)}) async-start(bf16[8,128,2048]{2,1,0:T(8,128)(2,1)} %stack.2), calls=%async_computation | async-start | bytes 8388608 | tf_op jit(solution)/shard_map/all_to_all | solution.py:57
  18.5 0.0 all-gather.5.cloned.1.call-start
  18.6 0.7 all-gather.5.cloned.1.call-update
  19.3 49.0 %all-to-all-done = bf16[8,128,2048]{2,1,0:T(8,128)(2,1)} async-done(((bf16[8,128,2048]{2,1,0:T(8,128)(2,1)}), bf16[8,128,2048]{2,1,0:T(8,128)(2,1)}, u32[]{:S(2)}, u32[]{:S(2)}) %all-to-all-start) | async-done | bytes 4194336 | tf_op jit(solution)/shard_map/all_to_all | solution.py:57
  68.3 55.4 %all-gather.3.cloned.1.call-done = bf16[2048,4096]{1,0:T(8,128)(2,1)} async-done(((bf16[128,4096]{1,0:T(8,128)(2,1)}), bf16[2048,4096]{1,0:T(8,128)(2,1)}) %all-gather.3.cloned.1.call-update) | async-done | bytes 16777232 | tf_op jit(solution)/shard_map/all_gather | solution.py:14
  123.7 13.0 %fusion.8 = (f32[1024]{0:T(1024)S(1)}, f32[2048]{0:T(1024)S(1)}) fusion(bf16[1024,2048]{1,0:T(8,128)(2,1)} %bitcast, bf16[2048,4096]{1,0:T(8,128)(2,1)} %all-gather.3.cloned.1.call-done), kind=kOutput, calls=%fused_computation.13 | convolution fusion | flops 8602514432 | bytes 12595200 | tf_op jit(solution)/shard_map/dot_general | solution.py:39
  136.7 0.6 broadcast_multiply_fusion.1
  137.3 4.4 %all-to-all-start.3 = ((f32[8,1,128]{2,1,0:T(1,128)}), f32[8,1,128]{2,1,0:T(1,128)S(1)}, u32[]{:S(2)}, u32[]{:S(2)}) async-start(f32[8,1,128]{2,1,0:T(1,128)} %bitcast.5), calls=%async_computation.3 | async-start | bytes 8192 | tf_op jit(solution)/shard_map/all_to_all | solution.py:28
  141.7 13.4 %fusion.1 = f32[2048]{0:T(1024)S(1)} fusion(bf16[1024,2048]{1,0:T(8,128)(2,1)} %bitcast, bf16[2048,4096]{1,0:T(8,128)(2,1)} %all-gather.3.cloned.1.call-done, s32[2048]{0:T(1024)S(1)} %iota_add_fusion, s32[1024]{0:T(1024)S(1)} %fusion.22), kind=kOutput, calls=%fused_computation.6 | convolution fusion | flops 8604612608 | bytes 12603392 | tf_op jit(solution)/shard_map/dot_general | solution.py:39
  155.2 2.3 all-gather.5.cloned.1.call-done
  157.5 13.3 %fusion = f32[2048]{0:T(1024)S(1)} fusion(bf16[1024,2048]{1,0:T(8,128)(2,1)} %all-gather.5.cloned.1.call-done, bf16[2048,4096]{1,0:T(8,128)(2,1)} %all-gather.3.cloned.1.call-done, s32[2048]{0:T(1024)S(1)} %iota_add_fusion, s32[1024]{0:T(1024)S(1)} %fusion.22), kind=kOutput, calls=%fused_computation.5 | convolution fusion | flops 8604612608 | bytes 12603392 | tf_op jit(solution)/shard_map/dot_general | solution.py:39
  170.8 0.6 broadcast_multiply_fusion
  171.4 0.0 all-to-all-done.3
  171.4 6.8 %all-to-all-start.2 = ((f32[16,1,128]{2,1,0:T(1,128)}), f32[16,1,128]{2,1,0:T(1,128)S(1)}, u32[]{:S(2)}, u32[]{:S(2)}) async-start(f32[16,1,128]{2,1,0:T(1,128)} %bitcast.3), calls=%async_computation.2 | async-start | bytes 16384 | tf_op jit(solution)/shard_map/all_to_all | solution.py:28
  178.2 0.6 multiply_subtract_fusion
  178.8 6.8 %all-to-all-done.2 = f32[16,1,128]{2,1,0:T(1,128)S(1)} async-done(((f32[16,1,128]{2,1,0:T(1,128)}), f32[16,1,128]{2,1,0:T(1,128)S(1)}, u32[]{:S(2)}, u32[]{:S(2)}) %all-to-all-start.2) | async-done | bytes 8224 | tf_op jit(solution)/shard_map/all_to_all | solution.py:28
  185.6 3.4 %all-to-all-start.1 = ((f32[16,1,128]{2,1,0:T(1,128)}), f32[16,1,128]{2,1,0:T(1,128)S(1)}, u32[]{:S(2)}, u32[]{:S(2)}) async-start(f32[16,1,128]{2,1,0:T(1,128)} %bitcast.1), calls=%async_computation.1 | async-start | bytes 16384 | tf_op jit(solution)/shard_map/all_to_all | solution.py:28
  189.1 7.5 %all-to-all-done.1 = f32[16,1,128]{2,1,0:T(1,128)S(1)} async-done(((f32[16,1,128]{2,1,0:T(1,128)}), f32[16,1,128]{2,1,0:T(1,128)S(1)}, u32[]{:S(2)}, u32[]{:S(2)}) %all-to-all-start.1) | async-done | bytes 8224 | tf_op jit(solution)/shard_map/all_to_all | solution.py:28
  196.5 0.6 fusion.24
  197.1 1.2 fusion.25
  199.7 9.0 %psum.28 = f32[]{:T(128)} all-reduce(f32[]{:T(128)S(6)} %add.79), channel_id=1, replica_groups=mesh['row_0'=4,'row_1'=2,'col_0'=4,'col_1'=4] {'row_0'}, use_global_device_ids=true, to_apply=%region_9.10 | all-reduce | flops 1 | bytes 8 | tf_op jit(solution)/shard_map/psum | solution.py:34
  208.7 3.1 %psum.29 = f32[]{:T(128)} all-reduce(f32[]{:T(128)} %psum.28), channel_id=1, replica_groups=mesh['row_0'=4,'row_1'=2,'col_0'=4,'col_1'=4] {'row_1'}, use_global_device_ids=true, to_apply=%region_10.11 | all-reduce | flops 1 | bytes 8 | tf_op jit(solution)/shard_map/psum | solution.py:34
  211.8 9.5 %psum.30 = f32[]{:T(128)} all-reduce(f32[]{:T(128)} %psum.29), channel_id=1, replica_groups=mesh['row_0'=4,'row_1'=2,'col_0'=4,'col_1'=4] {'col_0'}, use_global_device_ids=true, to_apply=%region_11.12 | all-reduce | flops 1 | bytes 8 | tf_op jit(solution)/shard_map/psum | solution.py:34
  221.2 9.5 %psum.31 = f32[]{:T(128)} all-reduce(f32[]{:T(128)} %psum.30), channel_id=1, replica_groups=mesh['row_0'=4,'row_1'=2,'col_0'=4,'col_1'=4] {'col_1'}, use_global_device_ids=true, to_apply=%region_12.13 | all-reduce | flops 1 | bytes 8 | tf_op jit(solution)/shard_map/psum | solution.py:34
  (4 shorter events, 0.1 us)
Async XLA Ops:
  7.2 116.5 %all-gather.3.cloned.1.call-start = ((), (), s32[]{:S(2)}) async-start(), calls=%async_computation.4 | async-start | bytes 17825792 | tf_op jit(solution)/shard_map/all_gather | solution.py:14
  13.1 55.2 %all-to-all-start = ((bf16[8,128,2048]{2,1,0:T(8,128)(2,1)}), bf16[8,128,2048]{2,1,0:T(8,128)(2,1)}, u32[]{:S(2)}, u32[]{:S(2)}) async-start(bf16[8,128,2048]{2,1,0:T(8,128)(2,1)} %stack.2), calls=%async_computation | async-start | bytes 8388608 | tf_op jit(solution)/shard_map/all_to_all | solution.py:57
  18.5 138.9 %all-gather.5.cloned.1.call-start = ((), (), s32[]{:S(2)}) async-start(), calls=%async_computation.5 | async-start | bytes 4718592 | tf_op jit(solution)/shard_map/all_gather | solution.py:62
  137.3 34.1 %all-to-all-start.3 = ((f32[8,1,128]{2,1,0:T(1,128)}), f32[8,1,128]{2,1,0:T(1,128)S(1)}, u32[]{:S(2)}, u32[]{:S(2)}) async-start(f32[8,1,128]{2,1,0:T(1,128)} %bitcast.5), calls=%async_computation.3 | async-start | bytes 8192 | tf_op jit(solution)/shard_map/all_to_all | solution.py:28
  171.4 14.2 %all-to-all-start.2 = ((f32[16,1,128]{2,1,0:T(1,128)}), f32[16,1,128]{2,1,0:T(1,128)S(1)}, u32[]{:S(2)}, u32[]{:S(2)}) async-start(f32[16,1,128]{2,1,0:T(1,128)} %bitcast.3), calls=%async_computation.2 | async-start | bytes 16384 | tf_op jit(solution)/shard_map/all_to_all | solution.py:28
  185.6 10.9 %all-to-all-start.1 = ((f32[16,1,128]{2,1,0:T(1,128)}), f32[16,1,128]{2,1,0:T(1,128)S(1)}, u32[]{:S(2)}, u32[]{:S(2)}) async-start(f32[16,1,128]{2,1,0:T(1,128)} %bitcast.1), calls=%async_computation.1 | async-start | bytes 16384 | tf_op jit(solution)/shard_map/all_to_all | solution.py:28
Sparse Core Ops, SparseCore 0:
  10.1 113.5 all-gather.2
  125.4 32.0 all-gather.4
